TPU v7x, 32 devices: a whole 2x2x4 slice. The times are simulated.
32 devices in a mesh: groups: 2 (over y), fsdp: 4 (over z), tensor: 4 (over x, core).
Axes of the slice: x: 2, y: 2, z: 4, core: 2. Of those that a mesh axis runs over, the one named last changes fastest.
Arguments:
- tokens: bfloat16 [2048, 4608], P(('groups', 'fsdp'), 'tensor'), parts along dimension 0, may hold values from -100 to 100
- norm_gain: bfloat16 [4608], P('tensor'), may hold values from 0.25 to 1.75
- w_query: bfloat16 [4608, 4096], P('fsdp', 'tensor'), may hold values from -0.5 to 0.5
- w_key: bfloat16 [4608, 2048], P('fsdp', 'tensor'), may hold values from -0.09375 to 0.09375
- w_value: bfloat16 [4608, 2048], P('fsdp', 'tensor'), may hold values from -0.09375 to 0.09375
- w_out: bfloat16 [4096, 4608], P('tensor', 'fsdp'), may hold values from -0.5 to 0.5
- post_gain: bfloat16 [4608], P('tensor'), may hold values from 0.25 to 1.75
Outputs:
- mixed: float32 [2048, 4608], P(('groups', 'fsdp'), 'tensor'), parts along dimension 0
There are 2 independent parts, one for each index of `groups`. A program takes and returns all parts, laid end to end along the dimension named above; an argument that names none is the same for every part. Nothing has to cross between parts.
All inputs are finite; a program needn't handle non-finite values.
Results may differ from a plain program's by a relative error of at most 0.0053.
Values may be sent and summed in bfloat16 or wider, within the bound.
A program may use at most 128 MiB of HBM per device.

v0:
```python
import functools

import jax
import jax.numpy as jnp
from jax import lax
from jax.experimental import pallas as pl
from jax.experimental.pallas import tpu as pltpu
from jax.sharding import PartitionSpec as P

HEAD_DIM = 128

eps_norm = 1e-06
soft_cap = 50.0
attn_scale = 144.0 ** (-0.5)
rope_base = 10000.0


def rotate(values, position):
    head_dim = values.shape[-1]
    half = head_dim // 2
    freq = rope_base ** (-(jnp.arange(half, dtype=jnp.float32) * 2.0 / head_dim))
    angle = position.astype(jnp.float32)[:, None] * freq[None, :]
    cosine = jnp.cos(angle)[:, None, :]
    sine = jnp.sin(angle)[:, None, :]
    first = values[..., :half]
    second = values[..., half:]
    return jnp.concatenate(
        [first * cosine - second * sine, second * cosine + first * sine], axis=-1
    )


def attend(query, keys, values, position):
    count, heads, head_dim = query.shape
    kv_count = keys.shape[1]
    grouped = query.reshape(count, kv_count, heads // kv_count, head_dim)
    scores = (
        jnp.einsum("nkgd,mkd->kgnm", grouped, keys, preferred_element_type=jnp.float32) * attn_scale
    )
    capped = soft_cap * jnp.tanh(scores / soft_cap)
    allowed = position[None, :] <= position[:, None]
    weights = jnp.where(allowed, jnp.exp(capped), 0.0)
    probs = (weights / jnp.sum(weights, axis=-1, keepdims=True)).astype(jnp.bfloat16)
    mixed = jnp.einsum("kgnm,mkd->nkgd", probs, values, preferred_element_type=jnp.float32)
    return mixed.reshape(count, heads * head_dim).astype(jnp.bfloat16)


def swap_pairs(n_fsdp, n_tensor, turn):
    ratio = n_fsdp // n_tensor
    pairs = []
    for f in range(n_fsdp):
        for t in range(n_tensor):
            j = (f + turn) % ratio
            pairs.append((f * n_tensor + t, (t * ratio + j) * n_tensor + f // ratio))
    return pairs


def to_rows(block, n_fsdp, n_tensor):
    rows = block.shape[0]
    ratio = n_fsdp // n_tensor
    width = block.shape[1] // ratio
    f = lax.axis_index("fsdp")
    if ratio == 1:
        held = lax.ppermute(block, ("fsdp", "tensor"), swap_pairs(n_fsdp, n_tensor, 0))
    else:
        held = jnp.zeros((ratio, rows, width), block.dtype)
        for turn in range(ratio):
            piece = lax.dynamic_slice_in_dim(block, (f + turn) % ratio * width, width, 1)
            got = lax.ppermute(piece, ("fsdp", "tensor"), swap_pairs(n_fsdp, n_tensor, turn))
            held = lax.dynamic_update_index_in_dim(held, got, (f - turn) % ratio, 0)
        held = held.reshape(ratio * rows, width)
    return lax.all_gather(held, "tensor", axis=0, tiled=True)


def from_rows(summed, rows, n_fsdp, n_tensor):
    ratio = n_fsdp // n_tensor
    width = summed.shape[1]
    f = lax.axis_index("fsdp")
    back = lambda turn: [(b, a) for a, b in swap_pairs(n_fsdp, n_tensor, turn)]
    if ratio == 1:
        return lax.ppermute(summed, ("fsdp", "tensor"), back(0))
    pieces = summed.reshape(ratio, rows, width)
    out = jnp.zeros((rows, ratio * width), summed.dtype)
    for turn in range(ratio):
        piece = lax.dynamic_index_in_dim(pieces, (f - turn) % ratio, 0, keepdims=False)
        got = lax.ppermute(piece, ("fsdp", "tensor"), back(turn))
        out = lax.dynamic_update_slice_in_dim(out, got, (f + turn) % ratio * width, 1)
    return out


MESH = pl.DeviceIdType.MESH
VMEM_LIMIT = 60 * 1024 * 1024


def greet(n, f, t):
    barrier = pltpu.get_barrier_semaphore()

    def signal(a, b):
        pl.semaphore_signal(
            barrier, inc=1, device_id={"fsdp": a, "tensor": b}, device_id_type=MESH
        )

    for k in range(1, n):
        signal(f, lax.rem(t + k, n))
    pl.when(f != t)(lambda: signal(t, f))
    pl.when(f > 0)(lambda: signal(f - 1, t))
    pl.when(f < n - 1)(lambda: signal(f + 1, t))
    one, none = jnp.int32(1), jnp.int32(0)
    peers = n - 1
    for there in (f != t, f > 0, f < n - 1):
        peers = peers + jnp.where(there, one, none)
    pl.semaphore_wait(barrier, peers)


def remote(src, dst, send, recv, a, b):
    return pltpu.make_async_remote_copy(
        src_ref=src,
        dst_ref=dst,
        send_sem=send,
        recv_sem=recv,
        device_id={"fsdp": a, "tensor": b},
        device_id_type=MESH,
    )


def qkv_kernel(
    n, cuts, sweeps, x_ref, wq_ref, wk_ref, wv_ref, out_ref,
    xs, from_low, from_high, stage,
    local_sem, turn_send, turn_recv, cast_send, cast_recv,
    up_send, up_recv, down_send, down_recv,
):
    f, t = lax.axis_index("fsdp"), lax.axis_index("tensor")
    rows = x_ref.shape[0]
    half = rows // cuts
    greet(n, f, t)

    def part_rows(h):
        start = h * half
        return pl.ds(start if isinstance(h, int) else pl.multiple_of(start, half), half)

    def turned(h, slot):
        return remote(
            x_ref.at[part_rows(h)], xs.at[slot, part_rows(h)],
            turn_send.at[h], turn_recv.at[h], t, f,
        )

    def kept():
        return pltpu.make_async_copy(x_ref, xs.at[t], local_sem)

    def cast(h, slot, k):
        return remote(
            xs.at[slot, part_rows(h)], xs.at[slot, part_rows(h)],
            cast_send.at[k - 1, h], cast_recv.at[slot, h], f, lax.rem(t + k, n),
        )

    @pl.when(f != t)
    def _():
        for h in range(cuts):
            turned(h, f).start()

    @pl.when(f == t)
    def _():
        kept().start()
        kept().wait()

    def spread(r):
        for i in range(cuts // sweeps):
            h = r * (cuts // sweeps) + i
            pl.when(f != t)(lambda h=h: turned(h, f).wait_recv())
            for k in range(1, n):
                cast(h, t, k).start()

    spread(0)

    span = rows // sweeps
    each = cuts // sweeps

    def arrive(slot, r):
        @pl.when(slot != t)
        def _():
            for h in range(each):
                cast(r * each + h, slot, 1).wait_recv()

    def swept(r):
        return pl.ds(pl.multiple_of(r * span, span), span)

    wide = wk_ref.shape[1]
    count = wq_ref.shape[1] // wide + 2
    weights = [(wq_ref, i * wide) for i in range(count - 2)] + [(wk_ref, 0), (wv_ref, 0)]

    def partial(block, c, r):
        ref, start = weights[c]
        return jnp.dot(
            xs[block, swept(r)],
            ref[:, start : start + wide],
            preferred_element_type=jnp.float32,
        )

    def up(d, c, r):
        return remote(
            stage.at[d, c, swept(r)], from_low.at[d, c, swept(r)],
            up_send.at[d, c, r], up_recv.at[d, c, r], lax.rem(f + 1, n), t,
        )

    def down(d, c, r):
        return remote(
            stage.at[d, c, swept(r)], from_high.at[d, c, swept(r)],
            down_send.at[d, c, r], down_recv.at[d, c, r], lax.rem(f + n - 1, n), t,
        )

    def widened(ref, d, c, r):
        return ref[d, c, swept(r)].astype(jnp.float32)

    def travel(d, c, r, copy, source, first):
        part = partial(d, c, r)

        @pl.when(first)
        def _():
            stage[d, c, swept(r)] = part.astype(stage.dtype)

        @pl.when(jnp.logical_not(first))
        def _():
            copy(d, c, r).wait_recv()
            stage[d, c, swept(r)] = (part + widened(source, d, c, r)).astype(stage.dtype)

        copy(d, c, r).start()

    def sweep(r, outer):
        def step(s, carry):
            high, low = n - 1 - s, s
            pl.when(high > f)(lambda: arrive(high, r))
            pl.when(low < f)(lambda: arrive(low, r))
            for c in range(count):
                pl.when(high > f)(lambda c=c: travel(high, c, r, up, from_low, f == 0))
                pl.when(low < f)(lambda c=c: travel(low, c, r, down, from_high, f == n - 1))
            pl.when((s == 0) & (r + 1 < sweeps))(lambda: spread(r + 1))
            return carry

        return lax.fori_loop(0, n - 1, step, outer)

    def finish(r, carry):
        arrive(f, r)
        for c in range(count):
            cols = slice(c * wide, (c + 1) * wide)
            out_ref[swept(r), cols] = partial(f, c, r)

            @pl.when(f > 0)
            def _():
                up(f, c, r).wait_recv()
                out_ref[swept(r), cols] += widened(from_low, f, c, r)

            @pl.when(f < n - 1)
            def _():
                down(f, c, r).wait_recv()
                out_ref[swept(r), cols] += widened(from_high, f, c, r)

        return carry

    lax.fori_loop(0, sweeps, sweep, 0)
    lax.fori_loop(0, sweeps, finish, 0)

    def drain(d, carry):
        for c in range(count):
            for r in range(sweeps):
                pl.when(d > f)(lambda c=c, r=r: up(d, c, r).wait_send())
                pl.when(d < f)(lambda c=c, r=r: down(d, c, r).wait_send())
        return carry

    lax.fori_loop(0, n, drain, 0)
    for h in range(cuts):
        pl.when(f != t)(lambda h=h: turned(h, f).wait_send())
        for k in range(1, n):
            cast(h, t, k).wait_send()


def out_kernel(
    n, cuts, kv, raw_ref, cos_ref, sin_ref, w_ref, out_ref,
    att, stage, got, merged, landed,
    up_send, up_recv, down_send, down_recv, plane_send, plane_recv, turn_send, turn_recv,
):
    f, t = lax.axis_index("fsdp"), lax.axis_index("tensor")
    rows = raw_ref.shape[0]
    half = rows // cuts
    greet(n, f, t)
    heads = w_ref.shape[0] // HEAD_DIM
    per = heads // kv

    def part_rows(r):
        return pl.ds(r * half, half)

    def up(src, r):
        return remote(
            att.at[src, part_rows(r)], att.at[src, part_rows(r)],
            up_send.at[src, r], up_recv.at[src, r], lax.rem(f + 1, n), t,
        )

    def down(src, r):
        return remote(
            att.at[src, part_rows(r)], att.at[src, part_rows(r)],
            down_send.at[src, r], down_recv.at[src, r], lax.rem(f + n - 1, n), t,
        )

    def turn_rows(u, span):
        other = pltpu.roll(u, HEAD_DIM // 2, 1)
        return (u * cos_ref[span] + other * sin_ref[span]).astype(jnp.bfloat16)

    def turn(u):
        return turn_rows(u, slice(0, rows))

    def piece(start):
        return raw_ref[:, start : start + HEAD_DIM]

    keys = [turn(piece((heads + h) * HEAD_DIM)) for h in range(kv)]
    values = [piece((heads + kv + h) * HEAD_DIM).astype(jnp.bfloat16) for h in range(kv)]
    for r in range(cuts):
        span, seen = slice(r * half, (r + 1) * half), (r + 1) * half
        query_at = r * half + lax.broadcasted_iota(jnp.int32, (half, seen), 0)
        allowed = lax.broadcasted_iota(jnp.int32, (half, seen), 1) <= query_at
        for g in range(heads):
            h = g // per
            query = turn_rows(piece(g * HEAD_DIM)[span], span)
            scores = lax.dot_general(
                query, keys[h][:seen], (((1,), (1,)), ((), ())),
                preferred_element_type=jnp.float32,
            ) * attn_scale
            capped = soft_cap * jnp.tanh(scores / soft_cap)
            e = jnp.where(allowed, jnp.exp(capped), 0.0)
            probs = (e / jnp.sum(e, axis=1, keepdims=True)).astype(jnp.bfloat16)
            mixed = jnp.dot(probs, values[h][:seen], preferred_element_type=jnp.float32)
            att[f, span, g * HEAD_DIM : (g + 1) * HEAD_DIM] = mixed.astype(jnp.bfloat16)
        pl.when(f < n - 1)(lambda r=r: up(f, r).start())
        pl.when(f > 0)(lambda r=r: down(f, r).start())

    def plane(d, r, slot):
        return remote(
            stage.at[d, part_rows(r)], got.at[slot, part_rows(r)],
            plane_send.at[d, r], plane_recv.at[slot, r], f, d,
        )

    def project(d, r):
        span = slice(r * half, (r + 1) * half)
        total = jnp.dot(att[d, span], w_ref[...], preferred_element_type=jnp.float32)
        stage[d, span] = total.astype(stage.dtype)
        pl.when(d != t)(lambda: plane(d, r, t).start())

    def step(s, r):
        low, high = f - s, f + s

        @pl.when(low >= 0)
        def _():
            up(low, r).wait_recv()
            pl.when(f < n - 1)(lambda: up(low, r).start())

        @pl.when(high < n)
        def _():
            down(high, r).wait_recv()
            pl.when(f > 0)(lambda: down(high, r).start())

        pl.when(low >= 0)(lambda: project(low, r))
        pl.when(high < n)(lambda: project(high, r))

    def back(r):
        return remote(
            merged.at[part_rows(r)], landed.at[part_rows(r)],
            turn_send.at[r], turn_recv.at[r], t, f,
        )

    def merge(r):
        span = slice(r * half, (r + 1) * half)
        total = stage[t, span].astype(jnp.float32)
        for k in range(1, n):
            slot = lax.rem(t + k, n)
            plane(slot, r, slot).wait_recv()
            total += got[slot, span].astype(jnp.float32)
        merged[span] = total.astype(merged.dtype)
        pl.when(f != t)(lambda: back(r).start())

    for r in range(cuts):
        project(f, r)
        for s in range(1, n):
            step(s, r)
            if s == 1 and r > 0:
                merge(r - 1)
    merge(cuts - 1)
    for r in range(cuts):
        span = slice(r * half, (r + 1) * half)

        @pl.when(f == t)
        def _():
            out_ref[span] = merged[span]

        @pl.when(f != t)
        def _():
            back(r).wait_recv()
            out_ref[span] = landed[span]
            back(r).wait_send()

    def drain(d, carry):
        for r in range(cuts):
            pl.when((d <= f) & (f < n - 1))(lambda r=r: up(d, r).wait_send())
            pl.when((d >= f) & (f > 0))(lambda r=r: down(d, r).wait_send())
            pl.when(d != t)(lambda r=r: plane(d, r, t).wait_send())
        return carry

    lax.fori_loop(0, n, drain, 0)


def in_vmem(count):
    return [pl.BlockSpec(memory_space=pltpu.VMEM)] * count


def project_in(n, normed, w_query, w_key, w_value):
    rows, width = normed.shape
    wide = w_key.shape[1]
    count = w_query.shape[1] // wide + 2
    cuts, sweeps = 4, 2
    block = (n, count, rows, wide)
    dma = pltpu.SemaphoreType.DMA
    return pl.pallas_call(
        functools.partial(qkv_kernel, n, cuts, sweeps),
        out_shape=jax.ShapeDtypeStruct((rows, count * wide), jnp.float32),
        in_specs=in_vmem(4),
        out_specs=pl.BlockSpec(memory_space=pltpu.VMEM),
        scratch_shapes=[
            pltpu.VMEM((n, rows, width), jnp.bfloat16),
            pltpu.VMEM(block, jnp.bfloat16),
            pltpu.VMEM(block, jnp.bfloat16),
            pltpu.VMEM(block, jnp.bfloat16),
            dma(()), dma((cuts,)), dma((cuts,)), dma((n - 1, cuts)), dma((n, cuts)),
            *[dma((n, count, sweeps))] * 4,
        ],
        compiler_params=pltpu.CompilerParams(
            collective_id=0, has_side_effects=True, vmem_limit_bytes=VMEM_LIMIT
        ),
    )(normed, w_query, w_key, w_value)


def project_out(n, raw, cosine, sine, w_out, kv):
    rows = raw.shape[0]
    width = w_out.shape[1]
    cuts = 2
    dma = pltpu.SemaphoreType.DMA
    return pl.pallas_call(
        functools.partial(out_kernel, n, cuts, kv),
        out_shape=jax.ShapeDtypeStruct((rows, width), jnp.bfloat16),
        in_specs=in_vmem(4),
        out_specs=pl.BlockSpec(memory_space=pltpu.VMEM),
        scratch_shapes=[
            pltpu.VMEM((n, rows, w_out.shape[0]), jnp.bfloat16),
            pltpu.VMEM((n, rows, width), jnp.bfloat16),
            pltpu.VMEM((n, rows, width), jnp.bfloat16),
            pltpu.VMEM((rows, width), jnp.bfloat16),
            pltpu.VMEM((rows, width), jnp.bfloat16),
            *[dma((n, cuts))] * 4,
            dma((n, cuts)), dma((n, cuts)), dma((cuts,)), dma((cuts,)),
        ],
        compiler_params=pltpu.CompilerParams(
            collective_id=1, has_side_effects=True, vmem_limit_bytes=VMEM_LIMIT
        ),
    )(raw, cosine, sine, w_out)


def tables(rows):
    half = HEAD_DIM // 2
    freq = rope_base ** (-(jnp.arange(half, dtype=jnp.float32) * 2.0 / HEAD_DIM))
    angle = jnp.arange(rows, dtype=jnp.int32).astype(jnp.float32)[:, None] * freq[None, :]
    cosine, sine = jnp.cos(angle), jnp.sin(angle)
    return jnp.concatenate([cosine, cosine], axis=1), jnp.concatenate([-sine, sine], axis=1)


def solution(mesh):
    n_fsdp, n_tensor = mesh.shape["fsdp"], mesh.shape["tensor"]

    def on_device(tokens, norm_gain, w_query, w_key, w_value, w_out, post_gain):
        rows = tokens.shape[0]
        width = tokens.shape[1] * n_tensor
        widened = tokens.astype(jnp.float32)
        total = lax.psum(jnp.sum(widened * widened, axis=1), "tensor")
        normed = (
            widened * lax.rsqrt(total / width + eps_norm)[:, None] * norm_gain.astype(jnp.float32)
        ).astype(jnp.bfloat16)
        if n_fsdp == n_tensor:
            kv = w_key.shape[1] // HEAD_DIM
            raw = project_in(n_fsdp, normed, w_query, w_key, w_value)
            proj = project_out(n_fsdp, raw, *tables(rows), w_out, kv).astype(jnp.float32)
        else:
            mine = to_rows(normed, n_fsdp, n_tensor)
            raw = []
            for piece in (w_query, w_key, w_value):
                part = jnp.dot(mine, piece, preferred_element_type=jnp.float32).astype(jnp.bfloat16)
                parts = lax.all_to_all(part, "fsdp", 0, 0, tiled=True)
                parts = parts.reshape(n_fsdp, rows, piece.shape[1])
                raw.append(jnp.sum(parts.astype(jnp.float32), axis=0))
            query_raw, key_raw, value_raw = raw
            position = jnp.arange(rows, dtype=jnp.int32)
            local_heads = w_query.shape[1] // HEAD_DIM
            local_kv = w_key.shape[1] // HEAD_DIM
            query = rotate(query_raw.reshape(rows, local_heads, HEAD_DIM), position)
            key = rotate(key_raw.reshape(rows, local_kv, HEAD_DIM), position)
            query, key = query.astype(jnp.bfloat16), key.astype(jnp.bfloat16)
            value = value_raw.astype(jnp.bfloat16).reshape(rows, local_kv, HEAD_DIM)
            attn = attend(query, key, value, position)
            attn_all = lax.all_gather(attn, "fsdp", axis=0, tiled=True)
            part = jnp.dot(attn_all, w_out, preferred_element_type=jnp.float32).astype(jnp.bfloat16)
            summed = lax.psum_scatter(part, "tensor", scatter_dimension=0, tiled=True)
            proj = from_rows(summed, rows, n_fsdp, n_tensor).astype(jnp.float32)
        post_total = lax.psum(jnp.sum(proj * proj, axis=1), "tensor")
        branch = (
            proj
            * lax.rsqrt(post_total / width + eps_norm)[:, None]
            * post_gain.astype(jnp.float32)
        )
        return tokens.astype(jnp.float32) + branch

    placed = (
        P(("groups", "fsdp"), "tensor"),
        P("tensor"),
        P("fsdp", "tensor"),
        P("fsdp", "tensor"),
        P("fsdp", "tensor"),
        P("tensor", "fsdp"),
        P("tensor"),
    )
    return jax.shard_map(
        on_device,
        mesh=mesh,
        in_specs=placed,
        out_specs=P(("groups", "fsdp"), "tensor"),
        check_vma=False,
    )
```

profile of v0, /device:TPU:15, one launch (start us, length us, event | category | flops | bytes accessed | tf_op | source)
XLA Modules:
  0.0 213.3 jit_solution(8263771215529955943)
XLA Ops:
  0.0 0.0 copy-start
  0.0 0.5 fusion.5
  0.6 0.8 pad_maximum_fusion
  1.4 0.7 convert_element_type.30
  2.1 0.0 copy-done
  2.1 0.2 fusion.2
  2.3 5.7 %psum.14 = f32[256]{0:T(256)S(1)} all-reduce(f32[256]{0:T(256)S(1)} %fusion.2), channel_id=1, replica_groups=mesh['groups'=2,'fsdp'=4,'tensor'=4] {'tensor'}, use_global_device_ids=true, to_apply=%region_1.0 | all-reduce | flops 256 | bytes 2048 | tf_op jit(solution)/shard_map/psum | solution.py:477
  8.0 1.0 fusion.4.x_ref
  9.1 122.9 %shard_map.73.raw_ref = f32[256,2048]{1,0:T(8,128)} custom-call(bf16[256,1152]{1,0:T(8,128)(2,1)} %fusion.4.x_ref, bf16[1152,1024]{1,0:T(8,128)(2,1)} %wq_ref.1, bf16[1152,512]{1,0:T(8,128)(2,1)} %wk_ref.1, bf16[1152,512]{1,0:T(8,128)(2,1)} %wv_ref.1), custom_call_target="tpu_custom_call" | custom-call | tf_op jit(solution)/shard_map/pallas_call | solution.py:418
  132.0 0.0 copy-start.1
  132.0 72.6 %shard_map.74 = bf16[256,1152]{1,0:T(8,128)(2,1)} custom-call(f32[256,2048]{1,0:T(8,128)} %shard_map.73.raw_ref, f32[256,128]{1,0:T(8,128)} %get-tuple-element.8.cos_ref, f32[256,128]{1,0:T(8,128)} %get-tuple-element.9.sin_ref, bf16[1024,1152]{1,0:T(8,128)(2,1)} %w_ref.1), custom_call_target="tpu_custom_call" | custom-call | tf_op jit(solution)/shard_map/pallas_call | solution.py:442
  204.6 1.3 fusion
  205.8 5.1 %psum.15 = f32[256]{0:T(256)S(1)} all-reduce(f32[256]{0:T(256)S(1)} %fusion), channel_id=1, replica_groups=mesh['groups'=2,'fsdp'=4,'tensor'=4] {'tensor'}, use_global_device_ids=true, to_apply=%region_3.0 | all-reduce | flops 256 | bytes 2048 | tf_op jit(solution)/shard_map/psum | solution.py:506
  211.0 0.0 copy-done.1
  211.0 2.3 %convert_add_fusion = f32[256,1152]{1,0:T(8,128)} fusion(bf16[256,1152]{1,0:T(8,128)(2,1)S(1)} %copy-done, bf16[256,1152]{1,0:T(8,128)(2,1)} %shard_map.74, f32[1152]{0:T(1024)S(1)} %convert_element_type.34, f32[256]{0:T(256)S(1)} %add_rsqrt_fusion), kind=kLoop, calls=%fused_computation | loop fusion | flops 1474560 | bytes 2364928 | tf_op jit(solution)/shard_map/add | solution.py:512
  (5 shorter events, 0.0 us)
Async XLA Ops:
  0.0 2.1 copy-start
  132.0 79.0 %copy-start.1 = (bf16[1152]{0:T(1024)(128)(2,1)S(1)}, bf16[1152]{0:T(1024)(128)(2,1)}, u32[]{:S(2)}) copy-start(bf16[1152]{0:T(1024)(128)(2,1)} %param.13) | copy-start | bytes 6916
where the time goes:
time: 216 us; the launch traced here: 213 us
  Pallas kernels  196 us (91%)
  blocking collectives  10.8 us (5%)
  other arithmetic  6.92 us (3%)
    pallas_call x1, Pallas kernels, project_in(): pl.pallas_call(functools.partial(qkv_kernel, n, cuts, sweeps), out_shape=...  123 us
    pallas_call x1, Pallas kernels, project_out(): pl.pallas_call(functools.partial(out_kernel, n, cuts, kv), out_shape=jax....  72.6 us
    psum x1, blocking collectives, on_device(): total = lax.psum(jnp.sum(widened * widened, axis=1), 'tensor')  5.73 us
    psum x1, blocking collectives, on_device(): post_total = lax.psum(jnp.sum(proj * proj, axis=1), 'tensor')  5.12 us

commit v1 on v0

v1 whole, which is shorter than its diff:
```python
import functools

import jax
import numpy as np
import jax.numpy as jnp
from jax import lax
from jax.experimental import pallas as pl
from jax.experimental.pallas import tpu as pltpu
from jax.sharding import PartitionSpec as P

HEAD_DIM = 128

eps_norm = 1e-06
soft_cap = 50.0
attn_scale = 144.0 ** (-0.5)
rope_base = 10000.0


def rotate(values, position):
    head_dim = values.shape[-1]
    half = head_dim // 2
    freq = rope_base ** (-(jnp.arange(half, dtype=jnp.float32) * 2.0 / head_dim))
    angle = position.astype(jnp.float32)[:, None] * freq[None, :]
    cosine = jnp.cos(angle)[:, None, :]
    sine = jnp.sin(angle)[:, None, :]
    first = values[..., :half]
    second = values[..., half:]
    return jnp.concatenate(
        [first * cosine - second * sine, second * cosine + first * sine], axis=-1
    )


def attend(query, keys, values, position):
    count, heads, head_dim = query.shape
    kv_count = keys.shape[1]
    grouped = query.reshape(count, kv_count, heads // kv_count, head_dim)
    scores = (
        jnp.einsum("nkgd,mkd->kgnm", grouped, keys, preferred_element_type=jnp.float32) * attn_scale
    )
    capped = soft_cap * jnp.tanh(scores / soft_cap)
    allowed = position[None, :] <= position[:, None]
    weights = jnp.where(allowed, jnp.exp(capped), 0.0)
    probs = (weights / jnp.sum(weights, axis=-1, keepdims=True)).astype(jnp.bfloat16)
    mixed = jnp.einsum("kgnm,mkd->nkgd", probs, values, preferred_element_type=jnp.float32)
    return mixed.reshape(count, heads * head_dim).astype(jnp.bfloat16)


def swap_pairs(n_fsdp, n_tensor, turn):
    ratio = n_fsdp // n_tensor
    pairs = []
    for f in range(n_fsdp):
        for t in range(n_tensor):
            j = (f + turn) % ratio
            pairs.append((f * n_tensor + t, (t * ratio + j) * n_tensor + f // ratio))
    return pairs


def to_rows(block, n_fsdp, n_tensor):
    rows = block.shape[0]
    ratio = n_fsdp // n_tensor
    width = block.shape[1] // ratio
    f = lax.axis_index("fsdp")
    if ratio == 1:
        held = lax.ppermute(block, ("fsdp", "tensor"), swap_pairs(n_fsdp, n_tensor, 0))
    else:
        held = jnp.zeros((ratio, rows, width), block.dtype)
        for turn in range(ratio):
            piece = lax.dynamic_slice_in_dim(block, (f + turn) % ratio * width, width, 1)
            got = lax.ppermute(piece, ("fsdp", "tensor"), swap_pairs(n_fsdp, n_tensor, turn))
            held = lax.dynamic_update_index_in_dim(held, got, (f - turn) % ratio, 0)
        held = held.reshape(ratio * rows, width)
    return lax.all_gather(held, "tensor", axis=0, tiled=True)


def from_rows(summed, rows, n_fsdp, n_tensor):
    ratio = n_fsdp // n_tensor
    width = summed.shape[1]
    f = lax.axis_index("fsdp")
    back = lambda turn: [(b, a) for a, b in swap_pairs(n_fsdp, n_tensor, turn)]
    if ratio == 1:
        return lax.ppermute(summed, ("fsdp", "tensor"), back(0))
    pieces = summed.reshape(ratio, rows, width)
    out = jnp.zeros((rows, ratio * width), summed.dtype)
    for turn in range(ratio):
        piece = lax.dynamic_index_in_dim(pieces, (f - turn) % ratio, 0, keepdims=False)
        got = lax.ppermute(piece, ("fsdp", "tensor"), back(turn))
        out = lax.dynamic_update_slice_in_dim(out, got, (f + turn) % ratio * width, 1)
    return out


MESH = pl.DeviceIdType.MESH
VMEM_LIMIT = 60 * 1024 * 1024
CHAIN = 4
LAG = 2
GATHER_AT = 15


def remote(src, dst, send, recv, a, b):
    return pltpu.make_async_remote_copy(
        src_ref=src,
        dst_ref=dst,
        send_sem=send,
        recv_sem=recv,
        device_id={"fsdp": a, "tensor": b},
        device_id_type=MESH,
    )


def greet(n, f, t):
    barrier = pltpu.get_barrier_semaphore()
    for a in range(n):
        for b in range(n):
            @pl.when(jnp.logical_not((f == a) & (t == b)))
            def _():
                pl.semaphore_signal(
                    barrier, inc=1, device_id={"fsdp": a, "tensor": b}, device_id_type=MESH
                )
    return lambda: pl.semaphore_wait(barrier, n * n - 1)


def loop(low, high, body):
    def step(i, carry):
        body(i)
        return carry

    lax.fori_loop(low, high, step, 0)


def row_sums(squares):
    groups = squares.shape[1] // 128
    lanes = squares[:, :128]
    for i in range(1, groups):
        lanes = lanes + squares[:, i * 128 : (i + 1) * 128]
    row = jnp.sum(lanes.T, axis=0, keepdims=True)
    return jnp.broadcast_to(row, (8, squares.shape[0]))


def as_column(row):
    return jnp.broadcast_to(row[:1], (128, row.shape[1])).T


def block_kernel(
    n, tok_ref, gains_ref, cos_ref, sin_ref, wq_hbm, wk_hbm, wv_hbm, wo_hbm, out_ref,
    w_all, wo, xn, xs, relay_buf, ss_mine, ss_got,
    near_stage, far_stage, near_got, far_got, keys, values, att,
    part_stage, part_got, pair_stage, pair_got, sum_stage, proj, post_mine, post_got,
    w_sem, ss_send, ss_recv, src_send, relay_recv, relay_send,
    x_recv, mate_send, cross_send, near_send, near_recv, far_send, far_recv,
    att_send, att_recv, part_send, part_recv, pair_send, pair_recv, sum_send, sum_recv,
    post_send, post_recv,
):
    f, t = lax.axis_index("fsdp"), lax.axis_index("tensor")
    rows, width = tok_ref.shape
    half = rows // 2
    kv = w_all.shape[0]
    per = att.shape[3] // HEAD_DIM
    count = 4 * kv
    lanes = width // 128
    total_width = width * n
    finish_greeting = greet(n, f, t)

    upper = f // 2
    inward = f + 1 - 2 * upper
    outward = f - 1 + 2 * upper
    at_end = (f == 0) | (f == n - 1)
    in_middle = (f > 0) & (f < n - 1)
    plane, core = t // 2, t % 2
    mate = t + 1 - 2 * core
    cross = (t + n // 2) % n
    leads = core == f % 2
    owner = f == t

    def near(c):
        return c + upper * (n - 1 - 2 * c)

    def far(c):
        return n - 1 - c + upper * (2 * c - n + 1)

    def rows_at(start, size):
        return pl.ds(start if isinstance(start, int) else pl.multiple_of(start, size), size)

    def side(h):
        return rows_at(h * half, half)

    fetches = []
    for g in range(kv):
        for ref, first, size in (
            (wq_hbm, 0, per * HEAD_DIM),
            (wk_hbm, per * HEAD_DIM, HEAD_DIM),
            (wv_hbm, (per + 1) * HEAD_DIM, HEAD_DIM),
        ):
            fetches.append(
                pltpu.make_async_copy(
                    ref.at[:, pl.ds(g * size, size)],
                    w_all.at[g, :, pl.ds(first, size)],
                    w_sem.at[len(fetches)],
                )
            )
    fetches.append(pltpu.make_async_copy(wo_hbm, wo, w_sem.at[len(fetches)]))
    for fetch in fetches:
        fetch.start()

    tok = tok_ref[...].astype(jnp.float32)
    ss_mine[...] = row_sums(tok * tok)
    finish_greeting()

    def total_out(k, slot):
        return remote(
            ss_mine, ss_got.at[slot], ss_send.at[k - 1], ss_recv.at[slot], f, (t + k) % n
        )

    for k in range(1, n):
        total_out(k, t).start()
    total = ss_mine[...]
    for k in range(1, n):
        slot = (t + k) % n
        total_out(k, slot).wait_recv()
        total = total + ss_got[slot]
    scale = lax.rsqrt(as_column(total) / total_width + eps_norm)
    for i in range(lanes):
        cols = slice(i * 128, (i + 1) * 128)
        xn[:, cols] = (
            tok_ref[:, cols].astype(jnp.float32) * scale * gains_ref[0:1, cols]
        ).astype(jnp.bfloat16)

    @pl.when(owner)
    def _():
        xs[f] = xn[...]

    def direct():
        return remote(
            xn.at[side(plane)], xs.at[f, side(plane)],
            src_send.at[0], x_recv.at[f, plane], t, t,
        )

    def to_relay():
        return remote(
            xn.at[side(1 - plane)], relay_buf, src_send.at[1], relay_recv, f, cross
        )

    def relayed():
        return remote(
            relay_buf, xs.at[f, side(plane)], relay_send, x_recv.at[f, plane], cross, t
        )

    def to_mate(r, h):
        return remote(
            xs.at[r, side(h)], xs.at[r, side(h)], mate_send.at[r, h], x_recv.at[r, h], f, mate
        )

    def to_cross(r, h):
        return remote(
            xs.at[r, side(h)], xs.at[r, side(h)], cross_send.at[r, h], x_recv.at[r, h], f, cross
        )

    @pl.when(jnp.logical_not(owner))
    def _():
        to_relay().start()
        direct().start()

    @pl.when(owner)
    def _():
        for h in range(2):
            to_cross(f, h).start()
            to_mate(f, h).start()

    @pl.when(cross != f)
    def _():
        to_relay().wait_recv()
        relayed().start()

    def spread(r):
        @pl.when(leads)
        def _():
            @pl.when(r != f)
            def _():
                to_mate(r, plane).wait_recv()
                to_cross(r, plane).start()
                to_mate(r, plane).start()
                to_mate(r, 1 - plane).wait_recv()
                to_mate(r, 1 - plane).start()

            @pl.when((r == f) & jnp.logical_not(owner))
            def _():
                for h in range(2):
                    to_mate(r, h).wait_recv()
                    to_mate(r, h).start()

        @pl.when(jnp.logical_not(leads))
        def _():
            for h in range(2):
                to_mate(r, h).wait_recv()

    def place(k):
        j = k // kv
        return j // 2, j % 2, k % kv

    def partial(seq, h, g):
        return jnp.dot(xs[seq, side(h)], w_all[g], preferred_element_type=jnp.float32)

    def near_hop(k, recv):
        landing = near_got if recv is near_recv else far_got
        return remote(
            near_stage.at[k], landing.at[k], near_send.at[k], recv.at[k], inward, t
        )

    def far_hop(k):
        return remote(
            far_stage.at[k], far_got.at[k], far_send.at[k], far_recv.at[k], outward, t
        )

    def first_near(k):
        c, h, g = place(k)
        near_stage[k] = partial(near(c), h, g).astype(jnp.bfloat16)
        near_hop(k, near_recv).start()

    def middle_near(k):
        c, h, g = place(k)
        part = partial(near(c), h, g)
        near_hop(k, near_recv).wait_recv()
        near_stage[k] = (part + near_got[k].astype(jnp.float32)).astype(jnp.bfloat16)
        near_hop(k, far_recv).start()

    def middle_far(k):
        c, h, g = place(k)
        part = partial(far(c), h, g)
        far_hop(k).wait_recv()
        far_stage[k] = (part + far_got[k].astype(jnp.float32)).astype(jnp.bfloat16)
        far_hop(k).start()

    def share(s, h, g, there):
        return remote(
            att.at[s, g, side(h)], att.at[s, g, side(h)],
            att_send.at[s, h, g], att_recv.at[s, h, g], there, t,
        )

    def turn(u, span):
        other = pltpu.roll(u, HEAD_DIM // 2, 1)
        return (u * cos_ref[span] + other * sin_ref[span]).astype(jnp.bfloat16)

    def attend_piece(c, h, g):
        k = (c * 2 + h) * kv + g
        span, seen = slice(h * half, (h + 1) * half), (h + 1) * half
        part = partial(far(c), h, g)
        far_hop(k).wait_recv()
        raw = part + far_got[k].astype(jnp.float32)
        heads = [raw[:, i * HEAD_DIM : (i + 1) * HEAD_DIM] for i in range(per + 2)]
        keys[c, g, span] = turn(heads[per], span)
        values[c, g, span] = heads[per + 1].astype(jnp.bfloat16)
        query = jnp.concatenate([turn(u, span) for u in heads[:per]], axis=0)
        scores = lax.dot_general(
            query, keys[c, g, :seen], (((1,), (1,)), ((), ())),
            preferred_element_type=jnp.float32,
        )
        capped = soft_cap * jnp.tanh(scores * (attn_scale / soft_cap))
        index = lax.broadcasted_iota(jnp.int32, (half, seen), 0) + h * half
        allowed = lax.broadcasted_iota(jnp.int32, (half, seen), 1) <= index
        allowed = jnp.concatenate([allowed] * per, axis=0)
        e = jnp.where(allowed, jnp.exp(capped), 0.0)
        inverse = 1.0 / jnp.sum(e, axis=1, keepdims=True)
        probs = (e * inverse).astype(jnp.bfloat16)
        mixed = jnp.dot(probs, values[c, g, :seen], preferred_element_type=jnp.float32)
        for i in range(per):
            att[far(c), g, span, i * HEAD_DIM : (i + 1) * HEAD_DIM] = mixed[
                i * half : (i + 1) * half
            ].astype(jnp.bfloat16)
        share(far(c), h, g, inward).start()

    quarter, eighth = half // 2, half // 4

    def part_hop(s, h):
        m = 2 * s + h
        return remote(
            part_stage.at[m, rows_at((1 - core) * quarter, quarter)], part_got.at[m],
            part_send.at[m], part_recv.at[m], f, mate,
        )

    def pair_hop(s, h):
        m = 2 * s + h
        return remote(
            pair_stage.at[m], pair_got.at[m], pair_send.at[m], pair_recv.at[m], f, cross
        )

    def sum_hop(s, h):
        m = 2 * s + h
        piece = core * 2 + plane
        return remote(
            sum_stage.at[m], proj.at[rows_at(h * half + piece * eighth, eighth)],
            sum_send.at[m], sum_recv.at[h, piece], s, f,
        )

    def pair_sum(m, which):
        kept = part_stage[m, rows_at(core * quarter + which * eighth, eighth)]
        got = part_got[m, rows_at(which * eighth, eighth)]
        return kept.astype(jnp.float32) + got.astype(jnp.float32)

    def out_first(s, h):
        m = 2 * s + h
        acc = jnp.dot(att[s, 0, side(h)], wo[: per * HEAD_DIM], preferred_element_type=jnp.float32)
        for g in range(1, kv):
            acc = acc + jnp.dot(
                att[s, g, side(h)],
                wo[g * per * HEAD_DIM : (g + 1) * per * HEAD_DIM],
                preferred_element_type=jnp.float32,
            )
        part_stage[m] = acc.astype(jnp.bfloat16)
        part_hop(s, h).start()

    def out_second(s, h):
        m = 2 * s + h
        part_hop(s, h).wait_recv()
        pair_stage[m] = pair_sum(m, 1 - plane).astype(jnp.bfloat16)
        pair_hop(s, h).start()

    def out_third(s, h):
        m = 2 * s + h
        pair_hop(s, h).wait_recv()
        summed = pair_sum(m, plane) + pair_got[m].astype(jnp.float32)
        stays = (s == f) & owner

        @pl.when(stays)
        def _():
            start = h * half + (core * 2 + plane) * eighth
            proj[rows_at(start, eighth)] = summed.astype(jnp.bfloat16)

        @pl.when(jnp.logical_not(stays))
        def _():
            sum_stage[m] = summed.astype(jnp.bfloat16)
            sum_hop(s, h).start()

    def advance(i, where):
        out_first(*where(i))
        pl.when(i >= 1)(lambda: out_second(*where(i - 1)))
        pl.when(i >= 2)(lambda: out_third(*where(i - 2)))

    def flush(where):
        out_second(*where(2 * n - 1))
        out_third(*where(2 * n - 2))
        out_third(*where(2 * n - 1))

    @pl.when(at_end)
    def _():
        def where(i):
            j = i % n
            c = j // 2
            return jnp.where(i < n, far(c), near(c)), j % 2

        spread(near(0))
        for fetch in fetches[:-1]:
            fetch.wait()
        loop(0, count // 2, first_near)
        spread(near(1))
        loop(count // 2, count, first_near)
        fetches[-1].wait()
        spread(far(0))
        spread(far(1))

        def chunk(c):
            for h in range(2):
                loop(0, kv, lambda g: attend_piece(c, h, g))
                advance(2 * c + h, where)

        loop(0, 2, chunk)

        def gather(i):
            s, h = where(i)
            for g in range(kv):
                share(s, h, g, inward).wait_recv()
            advance(i, where)

        loop(n, 2 * n, gather)
        flush(where)

    @pl.when(in_middle)
    def _():
        def where(i):
            j = i // 2
            c = j // 2
            return jnp.where(i % 2 == 0, far(c), near(c)), j % 2

        for r in (near(1), near(0), far(1), far(0)):
            spread(r)
        for fetch in fetches:
            fetch.wait()

        def pass_on(m, seq, there):
            for k in (2 * m, 2 * m + 1):
                c, h, g = place(k)
                share(seq(c), h, g, there).wait_recv()
                share(seq(c), h, g, there).start()

        def step(s):
            pl.when(s < count)(lambda: middle_near(s))
            pl.when((s >= LAG) & (s < count + LAG))(lambda: middle_far(s - LAG))
            m = s - GATHER_AT
            pl.when((m >= 0) & (m < count // 2))(lambda: pass_on(m, far, inward))
            pl.when((m >= 1) & (m < count // 2 + 1))(lambda: pass_on(m - 1, near, outward))
            pl.when(m >= 1)(lambda: advance(m - 1, where))

        loop(0, GATHER_AT + 2 * n + 1, step)
        flush(where)

    def post_out(h, k, slot):
        return remote(
            post_mine.at[h], post_got.at[h, slot],
            post_send.at[h, k - 1], post_recv.at[h, slot], f, (t + k) % n,
        )

    for h in range(2):
        for piece in range(n):
            mine = owner & (core * 2 + plane == piece)

            @pl.when(jnp.logical_not(mine))
            def _():
                spot = proj.at[rows_at(h * half + piece * eighth, eighth)]
                remote(
                    spot, spot, sum_send.at[0], sum_recv.at[h, piece], f, t
                ).wait_recv()

        branch = proj[side(h)].astype(jnp.float32)
        post_mine[h] = row_sums(branch * branch)
        for k in range(1, n):
            post_out(h, k, t).start()
    for h in range(2):
        total = post_mine[h]
        for k in range(1, n):
            slot = (t + k) % n
            post_out(h, k, slot).wait_recv()
            total = total + post_got[h, slot]
        scale = lax.rsqrt(as_column(total) / total_width + eps_norm)
        for i in range(lanes):
            cols = slice(i * 128, (i + 1) * 128)
            out_ref[side(h), cols] = tok_ref[side(h), cols].astype(jnp.float32) + (
                proj[side(h), cols].astype(jnp.float32) * scale * gains_ref[1:2, cols]
            )

    for k in range(1, n):
        total_out(k, t).wait_send()
        for h in range(2):
            post_out(h, k, t).wait_send()

    @pl.when(jnp.logical_not(owner))
    def _():
        to_relay().wait_send()
        direct().wait_send()

    pl.when(cross != f)(lambda: relayed().wait_send())

    def drain(r):
        @pl.when(leads)
        def _():
            for h in range(2):
                to_mate(r, h).wait_send()
                pl.when(((r != f) & (h == plane)) | ((r == f) & owner))(
                    lambda: to_cross(r, h).wait_send()
                )

        for h in range(2):
            part_hop(r, h).wait_send()
            pair_hop(r, h).wait_send()
            pl.when(jnp.logical_not((r == f) & owner))(lambda: sum_hop(r, h).wait_send())
            sent = in_middle | (r == far(0)) | (r == far(1))

            @pl.when(sent)
            def _():
                for g in range(kv):
                    share(r, h, g, inward).wait_send()

    loop(0, n, drain)

    def drain_hops(k):
        near_hop(k, far_recv).wait_send()
        pl.when(in_middle)(lambda: far_hop(k).wait_send())

    loop(0, count, drain_hops)


def whole_block(n, tokens, gains, cosine, sine, w_query, w_key, w_value, w_out):
    rows, width = tokens.shape
    half, kv = rows // 2, w_key.shape[1] // HEAD_DIM
    per = w_query.shape[1] // w_key.shape[1]
    wide = (per + 2) * HEAD_DIM
    count = 4 * kv
    dma = pltpu.SemaphoreType.DMA
    bf16 = lambda *shape: pltpu.VMEM(shape, jnp.bfloat16)
    f32 = lambda *shape: pltpu.VMEM(shape, jnp.float32)
    vmem = pl.BlockSpec(memory_space=pltpu.VMEM)
    anywhere = pl.BlockSpec(memory_space=pl.ANY)
    return pl.pallas_call(
        functools.partial(block_kernel, n),
        out_shape=jax.ShapeDtypeStruct((rows, width), jnp.float32),
        in_specs=[vmem] * 4 + [anywhere] * 4,
        out_specs=vmem,
        scratch_shapes=[
            bf16(kv, width, wide), bf16(*w_out.shape), bf16(rows, width),
            bf16(n, rows, width), bf16(half, width), f32(8, rows), f32(n, 8, rows),
            bf16(count, half, wide), bf16(count, half, wide),
            bf16(count, half, wide), bf16(count, half, wide),
            bf16(2, kv, rows, HEAD_DIM), bf16(2, kv, rows, HEAD_DIM),
            bf16(n, kv, rows, per * HEAD_DIM),
            bf16(2 * n, half, width), bf16(2 * n, half // 2, width),
            bf16(2 * n, half // 4, width), bf16(2 * n, half // 4, width),
            bf16(2 * n, half // 4, width), bf16(rows, width),
            f32(2, 8, half), f32(2, n, 8, half),
            dma((3 * kv + 1,)), dma((n - 1,)), dma((n,)), dma((2,)), dma(()), dma(()),
            dma((n, 2)), dma((n, 2)), dma((n, 2)),
            dma((count,)), dma((count,)), dma((count,)), dma((count,)),
            dma((n, 2, kv)), dma((n, 2, kv)),
            dma((2 * n,)), dma((2 * n,)), dma((2 * n,)), dma((2 * n,)),
            dma((2 * n,)), dma((2, n)),
            dma((2, n - 1)), dma((2, n)),
        ],
        compiler_params=pltpu.CompilerParams(
            collective_id=0, has_side_effects=True, vmem_limit_bytes=VMEM_LIMIT
        ),
    )(tokens, gains, cosine, sine, w_query, w_key, w_value, w_out)


def tables(rows):
    half = HEAD_DIM // 2
    freq = np.float32(rope_base) ** (-(np.arange(half, dtype=np.float32) * np.float32(2.0 / HEAD_DIM)))
    angle = np.arange(rows, dtype=np.float32)[:, None] * freq[None, :].astype(np.float32)
    cosine, sine = np.cos(angle), np.sin(angle)
    return (
        jnp.asarray(np.concatenate([cosine, cosine], axis=1), jnp.float32),
        jnp.asarray(np.concatenate([-sine, sine], axis=1), jnp.float32),
    )


def solution(mesh):
    n_fsdp, n_tensor = mesh.shape["fsdp"], mesh.shape["tensor"]

    def on_device(tokens, norm_gain, w_query, w_key, w_value, w_out, post_gain):
        rows = tokens.shape[0]
        width = tokens.shape[1] * n_tensor
        if n_fsdp == n_tensor == CHAIN:
            gains = jnp.stack([norm_gain, post_gain]).astype(jnp.float32)
            return whole_block(
                n_fsdp, tokens, gains, *tables(rows), w_query, w_key, w_value, w_out
            )
        widened = tokens.astype(jnp.float32)
        total = lax.psum(jnp.sum(widened * widened, axis=1), "tensor")
        normed = (
            widened * lax.rsqrt(total / width + eps_norm)[:, None] * norm_gain.astype(jnp.float32)
        ).astype(jnp.bfloat16)
        mine = to_rows(normed, n_fsdp, n_tensor)
        raw = []
        for piece in (w_query, w_key, w_value):
            part = jnp.dot(mine, piece, preferred_element_type=jnp.float32).astype(jnp.bfloat16)
            parts = lax.all_to_all(part, "fsdp", 0, 0, tiled=True)
            parts = parts.reshape(n_fsdp, rows, piece.shape[1])
            raw.append(jnp.sum(parts.astype(jnp.float32), axis=0))
        query_raw, key_raw, value_raw = raw
        position = jnp.arange(rows, dtype=jnp.int32)
        local_heads = w_query.shape[1] // HEAD_DIM
        local_kv = w_key.shape[1] // HEAD_DIM
        query = rotate(query_raw.reshape(rows, local_heads, HEAD_DIM), position)
        key = rotate(key_raw.reshape(rows, local_kv, HEAD_DIM), position)
        query, key = query.astype(jnp.bfloat16), key.astype(jnp.bfloat16)
        value = value_raw.astype(jnp.bfloat16).reshape(rows, local_kv, HEAD_DIM)
        attn = attend(query, key, value, position)
        attn_all = lax.all_gather(attn, "fsdp", axis=0, tiled=True)
        part = jnp.dot(attn_all, w_out, preferred_element_type=jnp.float32).astype(jnp.bfloat16)
        summed = lax.psum_scatter(part, "tensor", scatter_dimension=0, tiled=True)
        proj = from_rows(summed, rows, n_fsdp, n_tensor).astype(jnp.float32)
        post_total = lax.psum(jnp.sum(proj * proj, axis=1), "tensor")
        branch = (
            proj
            * lax.rsqrt(post_total / width + eps_norm)[:, None]
            * post_gain.astype(jnp.float32)
        )
        return tokens.astype(jnp.float32) + branch

    placed = (
        P(("groups", "fsdp"), "tensor"),
        P("tensor"),
        P("fsdp", "tensor"),
        P("fsdp", "tensor"),
        P("fsdp", "tensor"),
        P("tensor", "fsdp"),
        P("tensor"),
    )
    return jax.shard_map(
        on_device,
        mesh=mesh,
        in_specs=placed,
        out_specs=P(("groups", "fsdp"), "tensor"),
        check_vma=False,
    )
```

time: 216 us -> 148 us (0.69); the launches traced: 213 us -> 148 us
  Pallas kernels: 196 us -> 143 us
  blocking collectives: 10.8 us -> 0 us
  other arithmetic: 6.92 us -> 0.61 us
  local copies, waits for them, and re-layouts: 0.01 us -> 3.74 us
    pallas_call x2 -> x1, Pallas kernels: 196 us -> 143 us  [whole_block(): pl.pallas_call(functools.partial(block_kernel, n), out_shape=jax.ShapeDty...]
    psum x2 -> x0, blocking collectives: 10.8 us -> none  [the longest x1 5.73 us: on_device(): total = lax.psum(jnp.sum(widened * widened, axis=1), 'tensor')]
    unnamed x4 -> x1, local copies, waits for them, and re-layouts: 0.01 us -> 2.36 us
    add x1 -> x0, other arithmetic: 2.34 us -> none  [on_device(): return tokens.astype(jnp.float32) + branch]
where the time goes in v1:
time: 148 us
  Pallas kernels  143 us (97%)
  local copies, waits for them, and re-layouts  3.74 us (3%)
    pallas_call x1, Pallas kernels, whole_block(): pl.pallas_call(functools.partial(block_kernel, n), out_shape=jax.ShapeDty...  143 us

profile of v1, /device:TPU:15, one launch (start us, length us, event | category | flops | bytes accessed | tf_op | source)
XLA Modules:
  0.0 147.6 jit_solution(2255339820028413952)
XLA Ops:
  0.0 0.7 stack.9
  0.7 0.7 stack.10
  1.4 0.6 maximum_convert_fusion.gains_ref
  2.0 143.2 %shard_map.91 = f32[256,1152]{1,0:T(8,128)} custom-call(bf16[256,1152]{1,0:T(8,128)(2,1)} %tok_ref.1, f32[2,1152]{1,0:T(2,128)} %maximum_convert_fusion.gains_ref, f32[256,128]{1,0:T(8,128)} %constant.4.clone.cos_ref, f32[256,128]{1,0:T(8,128)} %constant.5.clone.sin_ref, bf16[1152,1024]{1,0:T(8,128)(2,1)} %wq_hbm.1, bf16[1152,512]{1,0:T(8,128)(2,1)} %wk_hbm.1, ...), custom_call_target="tpu_custom_call" | custom-call | tf_op jit(solution)/shard_map/pallas_call | solution.py:589
  145.2 2.4 %copy.11 = f32[256,1152]{1,0:T(8,128)} copy(f32[256,1152]{1,0:T(8,128)} %shard_map.91) | data formatting | bytes 2359296

commit v2 on v1

--- a/solution.py
+++ b/solution.py
@@ -92,7 +92,10 @@
 VMEM_LIMIT = 60 * 1024 * 1024
 CHAIN = 4
 LAG = 2
-GATHER_AT = 15
+FAR_AT, FAR_PACE = 15, 2
+NEAR_AT, NEAR_PACE = 17, 2
+OUT_AT = 18
+ENTRY, OTHER, LAST = 0, 1, 2
 
 
 def remote(src, dst, send, recv, a, b):
@@ -140,8 +143,8 @@
 
 
 def block_kernel(
-    n, tok_ref, gains_ref, cos_ref, sin_ref, wq_hbm, wk_hbm, wv_hbm, wo_hbm, out_ref,
-    w_all, wo, xn, xs, relay_buf, ss_mine, ss_got,
+    n, tok_hbm, gain_hbm, post_hbm, cos_hbm, sin_hbm, wq_hbm, wk_hbm, wv_hbm, wo_hbm, out_ref,
+    tok_ref, gain_ref, post_ref, cos_ref, sin_ref, small_sem, w_all, wo, xn, xs, relay_buf, ss_mine, ss_got,
     near_stage, far_stage, near_got, far_got, keys, values, att,
     part_stage, part_got, pair_stage, pair_got, sum_stage, proj, post_mine, post_got,
     w_sem, ss_send, ss_recv, src_send, relay_recv, relay_send,
@@ -182,6 +185,17 @@
     def side(h):
         return rows_at(h * half, half)
 
+    small = [
+        pltpu.make_async_copy(source, target, small_sem.at[i])
+        for i, (source, target) in enumerate(
+            (
+                (tok_hbm, tok_ref), (gain_hbm, gain_ref), (post_hbm, post_ref),
+                (cos_hbm, cos_ref), (sin_hbm, sin_ref),
+            )
+        )
+    ]
+    for fetch in small:
+        fetch.start()
     fetches = []
     for g in range(kv):
         for ref, first, size in (
@@ -200,6 +214,8 @@
     for fetch in fetches:
         fetch.start()
 
+    for fetch in small[:2]:
+        fetch.wait()
     tok = tok_ref[...].astype(jnp.float32)
     ss_mine[...] = row_sums(tok * tok)
     finish_greeting()
@@ -220,76 +236,75 @@
     for i in range(lanes):
         cols = slice(i * 128, (i + 1) * 128)
         xn[:, cols] = (
-            tok_ref[:, cols].astype(jnp.float32) * scale * gains_ref[0:1, cols]
+            tok_ref[:, cols].astype(jnp.float32) * scale * gain_ref[cols].astype(jnp.float32)[None, :]
         ).astype(jnp.bfloat16)
 
     @pl.when(owner)
     def _():
         xs[f] = xn[...]
 
-    def direct():
-        return remote(
-            xn.at[side(plane)], xs.at[f, side(plane)],
-            src_send.at[0], x_recv.at[f, plane], t, t,
-        )
-
-    def to_relay():
-        return remote(
-            xn.at[side(1 - plane)], relay_buf, src_send.at[1], relay_recv, f, cross
-        )
-
-    def relayed():
-        return remote(
-            relay_buf, xs.at[f, side(plane)], relay_send, x_recv.at[f, plane], cross, t
+    fetches = small[2:] + fetches
+
+    def is_outer(r):
+        return (r == 0) | (r == n - 1)
+
+    quarter, eighth = half // 2, half // 4
+    away = jnp.logical_not(owner)
+    detours = jnp.logical_not(is_outer(f)) & (plane != upper)
+    relays = jnp.logical_not(is_outer(f)) & (plane == upper)
+
+    def direct(h):
+        return remote(
+            xn.at[side(h)], xs.at[f, side(h)], src_send.at[h], x_recv.at[f, h], t, t
+        )
+
+    def to_relay(h):
+        return remote(
+            xn.at[side(h)], relay_buf.at[h], src_send.at[h], relay_recv.at[h], f, cross
+        )
+
+    def relayed(h):
+        return remote(
+            relay_buf.at[h], xs.at[f, side(h)], relay_send.at[h], x_recv.at[f, h], cross, t
         )
 
     def to_mate(r, h):
-        return remote(
-            xs.at[r, side(h)], xs.at[r, side(h)], mate_send.at[r, h], x_recv.at[r, h], f, mate
-        )
+        spot = xs.at[r, side(h)]
+        return remote(spot, spot, mate_send.at[r, h], x_recv.at[r, h], f, mate)
 
     def to_cross(r, h):
-        return remote(
-            xs.at[r, side(h)], xs.at[r, side(h)], cross_send.at[r, h], x_recv.at[r, h], f, cross
-        )
-
-    @pl.when(jnp.logical_not(owner))
-    def _():
-        to_relay().start()
-        direct().start()
-
-    @pl.when(owner)
-    def _():
-        for h in range(2):
-            to_cross(f, h).start()
-            to_mate(f, h).start()
-
-    @pl.when(cross != f)
-    def _():
-        to_relay().wait_recv()
-        relayed().start()
-
-    def spread(r):
-        @pl.when(leads)
+        spot = xs.at[r, side(h)]
+        return remote(spot, spot, cross_send.at[r, h], x_recv.at[r, h], f, cross)
+
+    def send_away(h):
+        pl.when(away & jnp.logical_not(detours))(lambda: direct(h).start())
+        pl.when(detours)(lambda: to_relay(h).start())
+
+    def relay(h):
+        @pl.when(relays)
         def _():
-            @pl.when(r != f)
-            def _():
-                to_mate(r, plane).wait_recv()
-                to_cross(r, plane).start()
-                to_mate(r, plane).start()
-                to_mate(r, 1 - plane).wait_recv()
-                to_mate(r, 1 - plane).start()
-
-            @pl.when((r == f) & jnp.logical_not(owner))
-            def _():
-                for h in range(2):
-                    to_mate(r, h).wait_recv()
-                    to_mate(r, h).start()
-
-        @pl.when(jnp.logical_not(leads))
+            to_relay(h).wait_recv()
+            relayed(h).start()
+
+    def enters(r):
+        by_owner = is_outer(r) | (r // 2 == upper)
+        return leads & ((by_owner & owner) | jnp.logical_not(by_owner | owner))
+
+    def spread(r, h, roles=(ENTRY, OTHER, LAST)):
+        enter = enters(r)
+        parts = {ENTRY: enter, OTHER: leads & jnp.logical_not(enter), LAST: jnp.logical_not(leads)}
+        active = parts[roles[0]]
+        for role in roles[1:]:
+            active = active | parts[role]
+
+        @pl.when(active & jnp.logical_not(owner & (r == f)))
         def _():
-            for h in range(2):
-                to_mate(r, h).wait_recv()
+            to_mate(r, h).wait_recv()
+
+        if ENTRY in roles:
+            pl.when(enter)(lambda: to_cross(r, h).start())
+        if roles != (LAST,):
+            pl.when(active & leads)(lambda: to_mate(r, h).start())
 
     def place(k):
         j = k // kv
@@ -366,8 +381,6 @@
             ].astype(jnp.bfloat16)
         share(far(c), h, g, inward).start()
 
-    quarter, eighth = half // 2, half // 4
-
     def part_hop(s, h):
         m = 2 * s + h
         return remote(
@@ -445,18 +458,31 @@
             c = j // 2
             return jnp.where(i < n, far(c), near(c)), j % 2
 
-        spread(near(0))
+        for h in range(2):
+            send_away(h)
         for fetch in fetches[:-1]:
             fetch.wait()
-        loop(0, count // 2, first_near)
-        spread(near(1))
-        loop(count // 2, count, first_near)
+        @pl.when(owner)
+        def _():
+            for h in range(2):
+                spread(f, h)
+            for h in range(2):
+                to_cross(f, h).wait_send()
+
+        for h in range(2):
+            pl.when(away)(lambda h=h: spread(near(0), h))
+            loop(h * kv, (h + 1) * kv, first_near)
+        for h in range(2):
+            spread(far(0), h)
+            spread(near(1), h)
+            loop((2 + h) * kv, (3 + h) * kv, first_near)
+        for h in range(2):
+            spread(far(1), h, (ENTRY,))
         fetches[-1].wait()
-        spread(far(0))
-        spread(far(1))
 
         def chunk(c):
             for h in range(2):
+                pl.when(c == 1)(lambda h=h: spread(far(1), h, (OTHER, LAST)))
                 loop(0, kv, lambda g: attend_piece(c, h, g))
                 advance(2 * c + h, where)
 
@@ -478,26 +504,41 @@
             c = j // 2
             return jnp.where(i % 2 == 0, far(c), near(c)), j % 2
 
-        for r in (near(1), near(0), far(1), far(0)):
-            spread(r)
+        for h in range(2):
+            send_away(h)
         for fetch in fetches:
             fetch.wait()
-
-        def pass_on(m, seq, there):
-            for k in (2 * m, 2 * m + 1):
-                c, h, g = place(k)
-                share(seq(c), h, g, there).wait_recv()
-                share(seq(c), h, g, there).start()
+        for h in range(2):
+            spread(near(0), h)
+        relay(0)
+        spread(far(0), 0)
+        relay(1)
+        plan = (
+            (far(0), 1, (0, 2, 4)), (near(1), 0, (1, 4, 6)), (near(1), 1, (1, 5, 8)),
+            (far(1), 0, (1, 4, 8)), (far(1), 1, (2, 6, 10)),
+        )
+
+        def pass_on(k, seq, there):
+            c, h, g = place(k)
+            share(seq(c), h, g, there).wait_recv()
+            share(seq(c), h, g, there).start()
 
         def step(s):
+            for seq, h, steps in plan:
+                for role, at in enumerate(steps):
+                    pl.when(s == at)(lambda seq=seq, h=h, role=role: spread(seq, h, (role,)))
             pl.when(s < count)(lambda: middle_near(s))
             pl.when((s >= LAG) & (s < count + LAG))(lambda: middle_far(s - LAG))
-            m = s - GATHER_AT
-            pl.when((m >= 0) & (m < count // 2))(lambda: pass_on(m, far, inward))
-            pl.when((m >= 1) & (m < count // 2 + 1))(lambda: pass_on(m - 1, near, outward))
-            pl.when(m >= 1)(lambda: advance(m - 1, where))
-
-        loop(0, GATHER_AT + 2 * n + 1, step)
+            for j in range(FAR_PACE):
+                k = (s - FAR_AT) * FAR_PACE + j
+                pl.when((k >= 0) & (k < count))(lambda k=k: pass_on(k, far, inward))
+            for j in range(NEAR_PACE):
+                k = (s - NEAR_AT) * NEAR_PACE + j
+                pl.when((k >= 0) & (k < count))(lambda k=k: pass_on(k, near, outward))
+            m = s - OUT_AT
+            pl.when(m >= 0)(lambda: advance(m, where))
+
+        loop(0, OUT_AT + 2 * n, step)
         flush(where)
 
     def post_out(h, k, slot):
@@ -531,7 +572,7 @@
         for i in range(lanes):
             cols = slice(i * 128, (i + 1) * 128)
             out_ref[side(h), cols] = tok_ref[side(h), cols].astype(jnp.float32) + (
-                proj[side(h), cols].astype(jnp.float32) * scale * gains_ref[1:2, cols]
+                proj[side(h), cols].astype(jnp.float32) * scale * post_ref[cols].astype(jnp.float32)[None, :]
             )
 
     for k in range(1, n):
@@ -539,21 +580,15 @@
         for h in range(2):
             post_out(h, k, t).wait_send()
 
-    @pl.when(jnp.logical_not(owner))
-    def _():
-        to_relay().wait_send()
-        direct().wait_send()
-
-    pl.when(cross != f)(lambda: relayed().wait_send())
+    for h in range(2):
+        pl.when(away)(lambda: direct(h).wait_send())
+        pl.when(relays)(lambda: relayed(h).wait_send())
 
     def drain(r):
-        @pl.when(leads)
-        def _():
-            for h in range(2):
-                to_mate(r, h).wait_send()
-                pl.when(((r != f) & (h == plane)) | ((r == f) & owner))(
-                    lambda: to_cross(r, h).wait_send()
-                )
+        for h in range(2):
+            waited = owner & (r == f) & is_outer(r)
+            pl.when(enters(r) & jnp.logical_not(waited))(lambda: to_cross(r, h).wait_send())
+            pl.when(leads)(lambda: to_mate(r, h).wait_send())
 
         for h in range(2):
             part_hop(r, h).wait_send()
@@ -575,7 +610,7 @@
     loop(0, count, drain_hops)
 
 
-def whole_block(n, tokens, gains, cosine, sine, w_query, w_key, w_value, w_out):
+def whole_block(n, tokens, gain, post_gain, cosine, sine, w_query, w_key, w_value, w_out):
     rows, width = tokens.shape
     half, kv = rows // 2, w_key.shape[1] // HEAD_DIM
     per = w_query.shape[1] // w_key.shape[1]
@@ -585,15 +620,17 @@
     bf16 = lambda *shape: pltpu.VMEM(shape, jnp.bfloat16)
     f32 = lambda *shape: pltpu.VMEM(shape, jnp.float32)
     vmem = pl.BlockSpec(memory_space=pltpu.VMEM)
-    anywhere = pl.BlockSpec(memory_space=pl.ANY)
+    in_hbm = pl.BlockSpec(memory_space=pltpu.HBM)
     return pl.pallas_call(
         functools.partial(block_kernel, n),
-        out_shape=jax.ShapeDtypeStruct((rows, width), jnp.float32),
-        in_specs=[vmem] * 4 + [anywhere] * 4,
+        out_shape=pltpu.VMEM((rows, width), jnp.float32),
+        in_specs=[in_hbm] * 9,
         out_specs=vmem,
         scratch_shapes=[
+            bf16(rows, width), bf16(width), bf16(width), f32(rows, HEAD_DIM), f32(rows, HEAD_DIM),
+            dma((5,)),
             bf16(kv, width, wide), bf16(*w_out.shape), bf16(rows, width),
-            bf16(n, rows, width), bf16(half, width), f32(8, rows), f32(n, 8, rows),
+            bf16(n, rows, width), bf16(2, half, width), f32(8, rows), f32(n, 8, rows),
             bf16(count, half, wide), bf16(count, half, wide),
             bf16(count, half, wide), bf16(count, half, wide),
             bf16(2, kv, rows, HEAD_DIM), bf16(2, kv, rows, HEAD_DIM),
@@ -602,7 +639,7 @@
             bf16(2 * n, half // 4, width), bf16(2 * n, half // 4, width),
             bf16(2 * n, half // 4, width), bf16(rows, width),
             f32(2, 8, half), f32(2, n, 8, half),
-            dma((3 * kv + 1,)), dma((n - 1,)), dma((n,)), dma((2,)), dma(()), dma(()),
+            dma((3 * kv + 1,)), dma((n - 1,)), dma((n,)), dma((2,)), dma((2,)), dma((2,)),
             dma((n, 2)), dma((n, 2)), dma((n, 2)),
             dma((count,)), dma((count,)), dma((count,)), dma((count,)),
             dma((n, 2, kv)), dma((n, 2, kv)),
@@ -613,7 +650,7 @@
         compiler_params=pltpu.CompilerParams(
             collective_id=0, has_side_effects=True, vmem_limit_bytes=VMEM_LIMIT
         ),
-    )(tokens, gains, cosine, sine, w_query, w_key, w_value, w_out)
+    )(tokens, gain, post_gain, cosine, sine, w_query, w_key, w_value, w_out)
 
 
 def tables(rows):
@@ -634,9 +671,8 @@
         rows = tokens.shape[0]
         width = tokens.shape[1] * n_tensor
         if n_fsdp == n_tensor == CHAIN:
-            gains = jnp.stack([norm_gain, post_gain]).astype(jnp.float32)
             return whole_block(
-                n_fsdp, tokens, gains, *tables(rows), w_query, w_key, w_value, w_out
+                n_fsdp, tokens, norm_gain, post_gain, *tables(rows), w_query, w_key, w_value, w_out
             )
         widened = tokens.astype(jnp.float32)
         total = lax.psum(jnp.sum(widened * widened, axis=1), "tensor")

time: 148 us -> 130 us (0.88)
  Pallas kernels: 143 us -> 129 us
  local copies, waits for them, and re-layouts: 3.74 us -> 1.02 us
    pallas_call x1, Pallas kernels: 143 us -> 129 us  [whole_block(): pl.pallas_call(functools.partial(block_kernel, n), out_shape=pltpu.VMEM((...]
where the time goes in v2:
time: 130 us
  Pallas kernels  129 us (99%)
    pallas_call x1, Pallas kernels, whole_block(): pl.pallas_call(functools.partial(block_kernel, n), out_shape=pltpu.VMEM((...  129 us

profile of v2, /device:TPU:15, one launch (start us, length us, event | category | flops | bytes accessed | tf_op | source)
XLA Modules:
  0.0 129.8 jit_solution(11272585142406383121)
XLA Ops:
  0.0 128.8 %shard_map.91 = f32[256,1152]{1,0:T(8,128)S(1)} custom-call(bf16[256,1152]{1,0:T(8,128)(2,1)} %tok_hbm.1, bf16[1152]{0:T(1024)(128)(2,1)} %gain_hbm.1, bf16[1152]{0:T(1024)(128)(2,1)} %post_hbm.1, f32[256,128]{1,0:T(8,128)} %constant.4.clone.cos_hbm, f32[256,128]{1,0:T(8,128)} %constant.5.clone.sin_hbm, bf16[1152,1024]{1,0:T(8,128)(2,1)} %wq_hbm.1, ...), custom_call_target="tpu_custom_call" | custom-call | tf_op jit(solution)/shard_map/pallas_call | solution.py:624
  128.8 1.0 copy.11

commit v3 on v2

--- a/solution.py
+++ b/solution.py
@@ -91,10 +91,12 @@
 MESH = pl.DeviceIdType.MESH
 VMEM_LIMIT = 60 * 1024 * 1024
 CHAIN = 4
-LAG = 2
-FAR_AT, FAR_PACE = 15, 2
+LAG = 3
+FAR_AT, FAR_RUSH = 15, 18
 NEAR_AT, NEAR_PACE = 17, 2
-OUT_AT = 18
+OUT_AT = 17
+EARLY = 2
+HOLD = 3
 ENTRY, OTHER, LAST = 0, 1, 2
 
 
@@ -441,16 +443,6 @@
             sum_stage[m] = summed.astype(jnp.bfloat16)
             sum_hop(s, h).start()
 
-    def advance(i, where):
-        out_first(*where(i))
-        pl.when(i >= 1)(lambda: out_second(*where(i - 1)))
-        pl.when(i >= 2)(lambda: out_third(*where(i - 2)))
-
-    def flush(where):
-        out_second(*where(2 * n - 1))
-        out_third(*where(2 * n - 2))
-        out_third(*where(2 * n - 1))
-
     @pl.when(at_end)
     def _():
         def where(i):
@@ -458,23 +450,24 @@
             c = j // 2
             return jnp.where(i < n, far(c), near(c)), j % 2
 
-        for h in range(2):
-            send_away(h)
-        for fetch in fetches[:-1]:
-            fetch.wait()
         @pl.when(owner)
         def _():
             for h in range(2):
                 spread(f, h)
-            for h in range(2):
-                to_cross(f, h).wait_send()
-
+
+        send_away(0)
+        for fetch in fetches[:-1]:
+            fetch.wait()
+        pl.when(owner)(lambda: to_cross(f, 0).wait_send())
+        pl.when(away)(lambda: spread(near(0), 0))
+        loop(0, EARLY, first_near)
+        send_away(1)
+        loop(EARLY, kv, first_near)
+        pl.when(away)(lambda: spread(near(0), 1))
+        loop(kv, 2 * kv, first_near)
         for h in range(2):
-            pl.when(away)(lambda h=h: spread(near(0), h))
-            loop(h * kv, (h + 1) * kv, first_near)
-        for h in range(2):
+            spread(near(1), h)
             spread(far(0), h)
-            spread(near(1), h)
             loop((2 + h) * kv, (3 + h) * kv, first_near)
         for h in range(2):
             spread(far(1), h, (ENTRY,))
@@ -484,18 +477,24 @@
             for h in range(2):
                 pl.when(c == 1)(lambda h=h: spread(far(1), h, (OTHER, LAST)))
                 loop(0, kv, lambda g: attend_piece(c, h, g))
-                advance(2 * c + h, where)
+                i = 2 * c + h
+                out_first(*where(i))
+                pl.when(i >= 1)(lambda: out_second(*where(i - 1)))
 
         loop(0, 2, chunk)
+
+        out_second(*where(n - 1))
 
         def gather(i):
             s, h = where(i)
             for g in range(kv):
                 share(s, h, g, inward).wait_recv()
-            advance(i, where)
+            out_first(s, h)
+            pl.when(i == n + HOLD)(lambda: loop(0, n, lambda j: out_third(*where(j))))
+            out_second(s, h)
+            out_third(s, h)
 
         loop(n, 2 * n, gather)
-        flush(where)
 
     @pl.when(in_middle)
     def _():
@@ -508,14 +507,11 @@
             send_away(h)
         for fetch in fetches:
             fetch.wait()
-        for h in range(2):
-            spread(near(0), h)
-        relay(0)
-        spread(far(0), 0)
-        relay(1)
+        spread(near(0), 0)
         plan = (
-            (far(0), 1, (0, 2, 4)), (near(1), 0, (1, 4, 6)), (near(1), 1, (1, 5, 8)),
-            (far(1), 0, (1, 4, 8)), (far(1), 1, (2, 6, 10)),
+            (far(0), 0, (0, 1, 2)), (near(0), 1, (2, 3, 4)), (far(0), 1, (2, 4, 5)),
+            (near(1), 0, (1, 3, 5)), (far(1), 0, (2, 5, 8)),
+            (near(1), 1, (3, 6, 8)), (far(1), 1, (3, 6, 10)),
         )
 
         def pass_on(k, seq, there):
@@ -524,22 +520,31 @@
             share(seq(c), h, g, there).start()
 
         def step(s):
+            for h in range(2):
+                pl.when(s == h)(lambda h=h: relay(h))
             for seq, h, steps in plan:
                 for role, at in enumerate(steps):
                     pl.when(s == at)(lambda seq=seq, h=h, role=role: spread(seq, h, (role,)))
+            pl.when((s >= LAG) & (s < count + LAG))(lambda: middle_far(s - LAG))
             pl.when(s < count)(lambda: middle_near(s))
-            pl.when((s >= LAG) & (s < count + LAG))(lambda: middle_far(s - LAG))
-            for j in range(FAR_PACE):
-                k = (s - FAR_AT) * FAR_PACE + j
-                pl.when((k >= 0) & (k < count))(lambda k=k: pass_on(k, far, inward))
+            late = jnp.maximum(s - FAR_RUSH, 0)
+            for j in range(3):
+                k = (s - FAR_AT) * 2 + late + j
+                due = (s >= FAR_AT) & (k < count)
+                if j == 2:
+                    due = due & (s >= FAR_RUSH)
+                pl.when(due)(lambda k=k: pass_on(k, far, inward))
+            m = s - OUT_AT
+            pl.when(m >= 1)(lambda: out_second(*where(m - 1)))
             for j in range(NEAR_PACE):
                 k = (s - NEAR_AT) * NEAR_PACE + j
                 pl.when((k >= 0) & (k < count))(lambda k=k: pass_on(k, near, outward))
-            m = s - OUT_AT
-            pl.when(m >= 0)(lambda: advance(m, where))
+            pl.when(m >= 0)(lambda: out_first(*where(m)))
 
         loop(0, OUT_AT + 2 * n, step)
-        flush(where)
+        loop(0, 2 * n - 1, lambda i: out_third(*where(i)))
+        out_second(*where(2 * n - 1))
+        out_third(*where(2 * n - 1))
 
     def post_out(h, k, slot):
         return remote(
@@ -586,7 +591,7 @@
 
     def drain(r):
         for h in range(2):
-            waited = owner & (r == f) & is_outer(r)
+            waited = owner & (r == f) & is_outer(r) & (h == 0)
             pl.when(enters(r) & jnp.logical_not(waited))(lambda: to_cross(r, h).wait_send())
             pl.when(leads)(lambda: to_mate(r, h).wait_send())
 

time: 130 us -> 124 us (0.954)
  Pallas kernels: 129 us -> 123 us
    pallas_call x1, Pallas kernels: 129 us -> 123 us  [whole_block(): pl.pallas_call(functools.partial(block_kernel, n), out_shape=pltpu.VMEM((...]
where the time goes in v3:
time: 124 us
  Pallas kernels  123 us (99%)
    pallas_call x1, Pallas kernels, whole_block(): pl.pallas_call(functools.partial(block_kernel, n), out_shape=pltpu.VMEM((...  123 us

profile of v3, /device:TPU:15, one launch (start us, length us, event | category | flops | bytes accessed | tf_op | source)
XLA Modules:
  0.0 123.7 jit_solution(7113568020532453116)
XLA Ops:
  0.0 122.6 %shard_map.91 = f32[256,1152]{1,0:T(8,128)S(1)} custom-call(bf16[256,1152]{1,0:T(8,128)(2,1)} %tok_hbm.1, bf16[1152]{0:T(1024)(128)(2,1)} %gain_hbm.1, bf16[1152]{0:T(1024)(128)(2,1)} %post_hbm.1, f32[256,128]{1,0:T(8,128)} %constant.4.clone.cos_hbm, f32[256,128]{1,0:T(8,128)} %constant.5.clone.sin_hbm, bf16[1152,1024]{1,0:T(8,128)(2,1)} %wq_hbm.1, ...), custom_call_target="tpu_custom_call" | custom-call | tf_op jit(solution)/shard_map/pallas_call | solution.py:629
  122.6 1.0 copy.11

commit v4 on v3

--- a/solution.py
+++ b/solution.py
@@ -146,10 +146,10 @@
 
 def block_kernel(
     n, tok_hbm, gain_hbm, post_hbm, cos_hbm, sin_hbm, wq_hbm, wk_hbm, wv_hbm, wo_hbm, out_ref,
-    tok_ref, gain_ref, post_ref, cos_ref, sin_ref, small_sem, w_all, wo, xn, xs, relay_buf, ss_mine, ss_got,
+    tok_ref, gain_ref, post_ref, cos_ref, sin_ref, small_sem, w_all, wo, xn, xs, relay_buf, ss_got, scales, gain_row,
     near_stage, far_stage, near_got, far_got, keys, values, att,
     part_stage, part_got, pair_stage, pair_got, sum_stage, proj, post_mine, post_got,
-    w_sem, ss_send, ss_recv, src_send, relay_recv, relay_send,
+    w_sem, held_sem, gain_send, gain_recv, ss_send, ss_recv, src_send, relay_recv, relay_send,
     x_recv, mate_send, cross_send, near_send, near_recv, far_send, far_recv,
     att_send, att_recv, part_send, part_recv, pair_send, pair_recv, sum_send, sum_recv,
     post_send, post_recv,
@@ -216,37 +216,15 @@
     for fetch in fetches:
         fetch.start()
 
+    fetches = small[2:] + fetches
+    held = pltpu.make_async_copy(tok_hbm, xs.at[f], held_sem)
+    pl.when(owner)(lambda: held.start())
     for fetch in small[:2]:
         fetch.wait()
     tok = tok_ref[...].astype(jnp.float32)
-    ss_mine[...] = row_sums(tok * tok)
+    ss_got[f, t] = row_sums(tok * tok)[:1]
+    pl.when(owner)(lambda: held.wait())
     finish_greeting()
-
-    def total_out(k, slot):
-        return remote(
-            ss_mine, ss_got.at[slot], ss_send.at[k - 1], ss_recv.at[slot], f, (t + k) % n
-        )
-
-    for k in range(1, n):
-        total_out(k, t).start()
-    total = ss_mine[...]
-    for k in range(1, n):
-        slot = (t + k) % n
-        total_out(k, slot).wait_recv()
-        total = total + ss_got[slot]
-    scale = lax.rsqrt(as_column(total) / total_width + eps_norm)
-    for i in range(lanes):
-        cols = slice(i * 128, (i + 1) * 128)
-        xn[:, cols] = (
-            tok_ref[:, cols].astype(jnp.float32) * scale * gain_ref[cols].astype(jnp.float32)[None, :]
-        ).astype(jnp.bfloat16)
-
-    @pl.when(owner)
-    def _():
-        xs[f] = xn[...]
-
-    fetches = small[2:] + fetches
-
     def is_outer(r):
         return (r == 0) | (r == n - 1)
 
@@ -257,12 +235,12 @@
 
     def direct(h):
         return remote(
-            xn.at[side(h)], xs.at[f, side(h)], src_send.at[h], x_recv.at[f, h], t, t
+            tok_ref.at[side(h)], xs.at[f, side(h)], src_send.at[h], x_recv.at[f, h], t, t
         )
 
     def to_relay(h):
         return remote(
-            xn.at[side(h)], relay_buf.at[h], src_send.at[h], relay_recv.at[h], f, cross
+            tok_ref.at[side(h)], relay_buf.at[h], src_send.at[h], relay_recv.at[h], f, cross
         )
 
     def relayed(h):
@@ -287,6 +265,53 @@
         def _():
             to_relay(h).wait_recv()
             relayed(h).start()
+
+    def total_out(a, b, c, d):
+        row = ss_got.at[c, d]
+        return remote(row, row, ss_send.at[a, b], ss_recv.at[c, d], a, b)
+
+    def gain_out(k):
+        return remote(
+            gain_row, gain_row, gain_send.at[k - 1], gain_recv, f, (t + k) % n
+        )
+
+    def elsewhere(a, b):
+        return jnp.logical_not((f == a) & (t == b))
+
+    def start_totals():
+        @pl.when(owner)
+        def _():
+            for i in range(lanes):
+                cols = slice(i * 128, (i + 1) * 128)
+                gain_row[:, cols] = gain_ref[cols].astype(jnp.float32)[None, :]
+            for k in range(1, n):
+                gain_out(k).start()
+
+        for a in range(n):
+            for b in range(n):
+                pl.when(elsewhere(a, b))(lambda a=a, b=b: total_out(a, b, f, t).start())
+
+    start_totals()
+
+    def finish_totals():
+        for r in range(n):
+            for b in range(n):
+                pl.when(elsewhere(r, b))(lambda r=r, b=b: total_out(r, b, r, b).wait_recv())
+            total = ss_got[r, 0]
+            for b in range(1, n):
+                total = total + ss_got[r, b]
+            scales[r] = lax.rsqrt(as_column(total) / total_width + eps_norm)
+        pl.when(away)(lambda: gain_out(1).wait_recv())
+
+    def normalise(r, h):
+        def group(i):
+            cols = rows_at(i * 128, 128)
+            wide = xs[r, side(h), cols].astype(jnp.float32)
+            xn[r, side(h), cols] = (
+                wide * scales[r, side(h)] * gain_row[:, cols]
+            ).astype(jnp.bfloat16)
+
+        loop(0, lanes, group)
 
     def enters(r):
         by_owner = is_outer(r) | (r // 2 == upper)
@@ -307,13 +332,14 @@
             pl.when(enter)(lambda: to_cross(r, h).start())
         if roles != (LAST,):
             pl.when(active & leads)(lambda: to_mate(r, h).start())
+        pl.when(active)(lambda: normalise(r, h))
 
     def place(k):
         j = k // kv
         return j // 2, j % 2, k % kv
 
     def partial(seq, h, g):
-        return jnp.dot(xs[seq, side(h)], w_all[g], preferred_element_type=jnp.float32)
+        return jnp.dot(xn[seq, side(h)], w_all[g], preferred_element_type=jnp.float32)
 
     def near_hop(k, recv):
         landing = near_got if recv is near_recv else far_got
@@ -450,12 +476,21 @@
             c = j // 2
             return jnp.where(i < n, far(c), near(c)), j % 2
 
+        send_away(0)
+
         @pl.when(owner)
         def _():
             for h in range(2):
-                spread(f, h)
-
-        send_away(0)
+                to_cross(f, h).start()
+                to_mate(f, h).start()
+
+        finish_totals()
+
+        @pl.when(owner)
+        def _():
+            for h in range(2):
+                normalise(f, h)
+
         for fetch in fetches[:-1]:
             fetch.wait()
         pl.when(owner)(lambda: to_cross(f, 0).wait_send())
@@ -505,6 +540,7 @@
 
         for h in range(2):
             send_away(h)
+        finish_totals()
         for fetch in fetches:
             fetch.wait()
         spread(near(0), 0)
@@ -580,8 +616,11 @@
                 proj[side(h), cols].astype(jnp.float32) * scale * post_ref[cols].astype(jnp.float32)[None, :]
             )
 
+    for a in range(n):
+        for b in range(n):
+            pl.when(elsewhere(a, b))(lambda: total_out(a, b, f, t).wait_send())
     for k in range(1, n):
-        total_out(k, t).wait_send()
+        pl.when(owner)(lambda: gain_out(k).wait_send())
         for h in range(2):
             post_out(h, k, t).wait_send()
 
@@ -634,8 +673,9 @@
         scratch_shapes=[
             bf16(rows, width), bf16(width), bf16(width), f32(rows, HEAD_DIM), f32(rows, HEAD_DIM),
             dma((5,)),
-            bf16(kv, width, wide), bf16(*w_out.shape), bf16(rows, width),
-            bf16(n, rows, width), bf16(2, half, width), f32(8, rows), f32(n, 8, rows),
+            bf16(kv, width, wide), bf16(*w_out.shape), bf16(n, rows, width),
+            bf16(n, rows, width), bf16(2, half, width), f32(n, n, 1, rows),
+            f32(n, rows, 128), f32(1, width),
             bf16(count, half, wide), bf16(count, half, wide),
             bf16(count, half, wide), bf16(count, half, wide),
             bf16(2, kv, rows, HEAD_DIM), bf16(2, kv, rows, HEAD_DIM),
@@ -644,7 +684,7 @@
             bf16(2 * n, half // 4, width), bf16(2 * n, half // 4, width),
             bf16(2 * n, half // 4, width), bf16(rows, width),
             f32(2, 8, half), f32(2, n, 8, half),
-            dma((3 * kv + 1,)), dma((n - 1,)), dma((n,)), dma((2,)), dma((2,)), dma((2,)),
+            dma((3 * kv + 1,)), dma(()), dma((n - 1,)), dma(()), dma((n, n)), dma((n, n)), dma((2,)), dma((2,)), dma((2,)),
             dma((n, 2)), dma((n, 2)), dma((n, 2)),
             dma((count,)), dma((count,)), dma((count,)), dma((count,)),
             dma((n, 2, kv)), dma((n, 2, kv)),

time: 124 us -> 122 us (0.984)
  Pallas kernels: 123 us -> 121 us
    pallas_call x1, Pallas kernels: 123 us -> 121 us  [whole_block(): pl.pallas_call(functools.partial(block_kernel, n), out_shape=pltpu.VMEM((...]
where the time goes in v4:
time: 122 us
  Pallas kernels  121 us (99%)
    pallas_call x1, Pallas kernels, whole_block(): pl.pallas_call(functools.partial(block_kernel, n), out_shape=pltpu.VMEM((...  121 us

profile of v4, /device:TPU:15, one launch (start us, length us, event | category | flops | bytes accessed | tf_op | source)
XLA Modules:
  0.0 121.7 jit_solution(16803544062141841498)
XLA Ops:
  0.0 120.7 %shard_map.91 = f32[256,1152]{1,0:T(8,128)S(1)} custom-call(bf16[256,1152]{1,0:T(8,128)(2,1)} %tok_hbm.1, bf16[1152]{0:T(1024)(128)(2,1)} %gain_hbm.1, bf16[1152]{0:T(1024)(128)(2,1)} %post_hbm.1, f32[256,128]{1,0:T(8,128)} %constant.4.clone.cos_hbm, f32[256,128]{1,0:T(8,128)} %constant.5.clone.sin_hbm, bf16[1152,1024]{1,0:T(8,128)(2,1)} %wq_hbm.1, ...), custom_call_target="tpu_custom_call" | custom-call | tf_op jit(solution)/shard_map/pallas_call | solution.py:668
  120.7 1.0 copy.11

commit v5 on v4

--- a/solution.py
+++ b/solution.py
@@ -95,7 +95,7 @@
 FAR_AT, FAR_RUSH = 15, 18
 NEAR_AT, NEAR_PACE = 17, 2
 OUT_AT = 17
-EARLY = 2
+EARLY = 3
 HOLD = 3
 ENTRY, OTHER, LAST = 0, 1, 2
 

time: 122 us -> 122 us (level)
  no operation moved by 1% of the time
where the time goes in v5:
time: 122 us
  Pallas kernels  121 us (99%)
    pallas_call x1, Pallas kernels, whole_block(): pl.pallas_call(functools.partial(block_kernel, n), out_shape=pltpu.VMEM((...  121 us

profile of v5, /device:TPU:15, one launch (start us, length us, event | category | flops | bytes accessed | tf_op | source)
XLA Modules:
  0.0 121.7 jit_solution(17315376935451478654)
XLA Ops:
  0.0 120.6 %shard_map.91 = f32[256,1152]{1,0:T(8,128)S(1)} custom-call(bf16[256,1152]{1,0:T(8,128)(2,1)} %tok_hbm.1, bf16[1152]{0:T(1024)(128)(2,1)} %gain_hbm.1, bf16[1152]{0:T(1024)(128)(2,1)} %post_hbm.1, f32[256,128]{1,0:T(8,128)} %constant.4.clone.cos_hbm, f32[256,128]{1,0:T(8,128)} %constant.5.clone.sin_hbm, bf16[1152,1024]{1,0:T(8,128)(2,1)} %wq_hbm.1, ...), custom_call_target="tpu_custom_call" | custom-call | tf_op jit(solution)/shard_map/pallas_call | solution.py:668
  120.6 1.0 copy.11
